TPU v7x, 32 devices: a whole 2x2x4 slice. The times are simulated.
32 devices in a mesh: blk: 16 (over z, x, core), cuts: 2 (over y).
Axes of the slice: x: 2, y: 2, z: 4, core: 2. Of those that a mesh axis runs over, the one named last changes fastest.
Arguments:
- left_env: bfloat16 [2048, 8, 2048], P('blk', 'cuts'), may hold values from -4 to 4
- right_env: bfloat16 [2048, 8, 2048], P('blk', 'cuts'), may hold values from -4 to 4
- left_core: float32 [8, 8, 2, 2], replicated, may hold values from -1.5 to 1.5
- right_core: float32 [8, 8, 2, 2], replicated, may hold values from -1.5 to 1.5
- slot_bond: int32 [8], replicated, may hold values from 0 to 7, each once
- krylov_basis: float32 [8, 2048, 4, 2048], P(None, 'blk', None, 'cuts'), may hold values from -30 to 30
- beta_prev: float32 [], replicated, may hold values from 0.3 to 1.2
Outputs:
- next_vector: float32 [2048, 4, 2048], P('blk', None, 'cuts')
- alpha_values: float32 [1], replicated
- beta_values: float32 [1], replicated
Inputs may be any that keep to these rules, and one draw needn't show every extreme that they name: `slot_bond`: a permutation of the 8 bond values.
All inputs are finite; a program needn't handle non-finite values.
Results may differ from a plain program's by a relative error of at most 0.00073.
The roundings to bfloat16 on the way count: a program that leaves them out, or rounds other values in their place, can miss the bound.
Values may be sent and summed in bfloat16 or wider, within the bound.
A program may use at most 192 MiB of HBM per device.

v0:
```python
import jax
import jax.numpy as jnp
from jax import lax
from jax.sharding import PartitionSpec as P


def build_table(left_core, right_core, slot_bond):
    bond_width = left_core.shape[0]
    phys_dim = left_core.shape[2]
    chosen = (slot_bond[:, None] == jnp.arange(bond_width, dtype=jnp.int32)[None, :]).astype(
        jnp.float32
    )
    picked = jnp.einsum("kw,wxac->kxac", chosen, left_core, precision=lax.Precision.HIGHEST)
    table = jnp.einsum("kxac,xybd->kyabcd", picked, right_core, precision=lax.Precision.HIGHEST)
    return table.reshape(bond_width, bond_width, phys_dim * phys_dim, phys_dim * phys_dim)


def on_device(left_env, right_env, left_core, right_core, slot_bond, krylov_basis, beta_prev):
    highest = lax.Precision.HIGHEST
    bond_width = left_core.shape[0]
    pair_count = left_core.shape[2] * left_core.shape[2]
    basis_count = krylov_basis.shape[0]
    row_count = krylov_basis.shape[1]
    col_count = krylov_basis.shape[3]
    full_width = left_env.shape[2]
    entries = float(full_width * pair_count * full_width)
    mpo_table = build_table(left_core, right_core, slot_bond)
    left_full = lax.all_gather(left_env, "cuts", axis=1, tiled=True)
    left_matrix = left_full.reshape(row_count * bond_width, full_width)
    right_local = lax.all_to_all(right_env, "cuts", split_axis=2, concat_axis=1, tiled=True)
    next_vector = krylov_basis[basis_count - 1]
    current_f = krylov_basis[basis_count - 1]
    previous = krylov_basis[basis_count - 2]
    current = current_f.astype(jnp.bfloat16)
    block_rows = lax.all_gather(current, "blk", axis=0, tiled=True)
    count_rows = block_rows.shape[0]
    projected = jnp.dot(
        left_matrix,
        block_rows.reshape(count_rows, pair_count * col_count),
        preferred_element_type=jnp.float32,
    )
    projected = projected.reshape(row_count, bond_width, pair_count, col_count)
    mixed_left = jnp.einsum("kypq,akqb->apyb", mpo_table, projected, precision=highest).astype(
        jnp.bfloat16
    )
    left_side = mixed_left.reshape(row_count * pair_count, bond_width * col_count)
    block_rows = lax.all_gather(right_local, "blk", axis=0, tiled=True)
    flat_rows = block_rows.reshape(block_rows.shape[0], -1)
    partial_terms = lax.dot_general(
        left_side, flat_rows, (((1,), (1,)), ((), ())), preferred_element_type=jnp.float32
    )
    image_vec = lax.psum_scatter(
        partial_terms.reshape(row_count, pair_count, full_width),
        "cuts",
        scatter_dimension=2,
        tiled=True,
    )
    local_gram = jnp.einsum("japb,kapb->jk", krylov_basis, krylov_basis, precision=highest)
    gram_matrix = lax.psum(local_gram, ("blk", "cuts")) / entries
    local_prods = jnp.einsum("japb,apb->j", krylov_basis, image_vec, precision=highest)
    inner_prods, image_square = lax.psum(
        (local_prods, jnp.sum(image_vec * image_vec)), ("blk", "cuts")
    )
    inner_prods = inner_prods / entries
    image_square = image_square / entries
    alpha_now = inner_prods[basis_count - 1]
    ortho_coeffs = (
        inner_prods
        - alpha_now * gram_matrix[:, basis_count - 1]
        - beta_prev * gram_matrix[:, basis_count - 2]
    )
    first_square = (
        image_square
        - 2.0 * alpha_now * inner_prods[basis_count - 1]
        - 2.0 * beta_prev * inner_prods[basis_count - 2]
        + alpha_now * alpha_now * gram_matrix[basis_count - 1, basis_count - 1]
        + 2.0 * alpha_now * beta_prev * gram_matrix[basis_count - 1, basis_count - 2]
        + beta_prev * beta_prev * gram_matrix[basis_count - 2, basis_count - 2]
    )
    square_mean = (
        first_square
        - 2.0 * jnp.sum(ortho_coeffs * ortho_coeffs)
        + jnp.sum(ortho_coeffs[:, None] * gram_matrix * ortho_coeffs[None, :])
    )
    first_pass = image_vec - alpha_now * current_f - beta_prev * previous
    second_pass = first_pass - jnp.einsum(
        "j,japb->apb", ortho_coeffs, krylov_basis, precision=highest
    )
    beta_new = jnp.sqrt(square_mean + 1e-06)
    next_vector = second_pass / beta_new
    alpha_list = [alpha_now]
    beta_list = [beta_new]
    return (next_vector, jnp.stack(alpha_list), jnp.stack(beta_list))


def solution(mesh):
    in_specs = (
        P("blk", "cuts", None),
        P("blk", "cuts", None),
        P(),
        P(),
        P(),
        P(None, "blk", None, "cuts"),
        P(),
    )
    out_specs = (P("blk", None, "cuts"), P(), P())
    return jax.shard_map(
        on_device, mesh=mesh, in_specs=in_specs, out_specs=out_specs, check_vma=False
    )
```

profile of v0, /device:TPU:0, one launch (start us, length us, event | category | flops | bytes accessed | tf_op | source)
XLA Modules:
  0.0 616.2 jit_solution(4557364010513093199)
XLA Ops:
  7.2 4.5 fusion.43
  11.7 1.3 copy-done.3
  13.1 2.1 copy.113
  15.2 0.0 all-gather.5.cloned.1.call-start
  15.2 2.5 copy.42
  17.8 0.0 all-gather.7.cloned.1.call-start
  17.8 5.6 copy.50
  23.4 30.2 %all_to_all.18 = bf16[128,4,2048]{0,1,2:T(4,128)(2,1)S(1)} all-to-all(bf16[128,4,2048]{0,1,2:T(4,128)(2,1)} %copy.50), channel_id=1, replica_groups=mesh['blk'=16,'cuts'=2] {'cuts'}, dimensions={2} | all-to-all | bytes 4194304 | tf_op jit(solution)/shard_map/all_to_all | solution.py:30
  53.6 2.7 copy.51
  56.3 0.0 reduce-scatter.2.cloned.1.call-start
  56.4 0.2 convolution_bitcast_fusion.1
  56.5 0.2 convolution_bitcast_fusion
  56.7 0.6 copy.48
  57.4 87.1 %all-gather.9.cloned.1.call-done = bf16[1,2048,4,1024]{3,1,2,0:T(8,128)(2,1)} async-done(((bf16[1,128,4,1024]{3,1,2,0:T(8,128)(2,1)}), bf16[1,2048,4,1024]{3,1,2,0:T(8,128)(2,1)}) %all-gather.9.cloned.1.call-update) | async-done | bytes 16777232 | tf_op jit(solution)/shard_map/all_gather | solution.py:35
  144.5 22.2 %copy.44 = bf16[1,2048,4,1024]{1,3,2,0:T(8,128)(2,1)} copy(bf16[1,2048,4,1024]{3,1,2,0:T(8,128)(2,1)} %all-gather.9.cloned.1.call-done) | data formatting | bytes 33554432 | tf_op jit(solution)/shard_map/all_gather | solution.py:35
  166.7 34.2 %all-gather.5.cloned.1.call-done = bf16[128,8,2048]{2,0,1:T(8,128)(2,1)} async-done(((bf16[128,4,2048]{2,0,1:T(8,128)(2,1)}), bf16[128,8,2048]{2,0,1:T(8,128)(2,1)}) %all-gather.5.cloned.1.call-update) | async-done | bytes 4194320 | tf_op jit(solution)/shard_map/all_gather | solution.py:28
  201.0 25.6 %fusion.4 = f32[128,8,4,1024]{3,1,2,0:T(8,128)} fusion(bf16[1,2048,4,1024]{1,3,2,0:T(8,128)(2,1)} %copy.44, bf16[128,8,2048,1]{2,0,1,3:T(8,128)(2,1)} %bitcast.94), kind=kOutput, calls=%fused_computation.4 | convolution fusion | flops 17179869184 | bytes 37748736 | tf_op jit(solution)/shard_map/dot_general | solution.py:37
  226.6 20.6 %fusion.15 = bf16[128,4,8,1024]{3,2,1,0:T(8,128)(2,1)} fusion(f32[8,8,4,4,1]{1,0,3,2,4:T(8,128)S(1)} %bitcast.93, f32[128,8,4,1024]{3,1,2,0:T(8,128)} %fusion.4), kind=kOutput, calls=%fused_computation.14 | convolution fusion | flops 1614807040 | bytes 25169920 | tf_op jit(solution)/shard_map/kypq,akqb->apyb/dot_general | solution.py:43
  247.2 123.4 %all-gather.7.cloned.1.call-done = bf16[2048,8,1024]{2,0,1:T(8,128)(2,1)} async-done(((bf16[128,8,1024]{2,0,1:T(8,128)(2,1)}), bf16[2048,8,1024]{2,0,1:T(8,128)(2,1)}) %all-gather.7.cloned.1.call-update) | async-done | bytes 33554448 | tf_op jit(solution)/shard_map/all_gather | solution.py:47
  370.6 46.7 %fusion.19 = f32[128,4,2048]{2,0,1:T(8,128)} fusion(bf16[2048,8,1024]{2,0,1:T(8,128)(2,1)} %all-gather.7.cloned.1.call-done, bf16[128,4,8,1024]{3,2,1,0:T(8,128)(2,1)} %fusion.15), kind=kOutput, calls=%fused_computation.16 | convolution fusion | flops 17179869184 | bytes 46137344 | tf_op jit(solution)/shard_map/dot_general | solution.py:49
  418.0 54.5 %fusion.29 = f32[8,8]{1,0:T(8,128)S(1)} fusion(f32[8,128,4,1024]{3,2,1,0:T(4,128)} %param.12), kind=kOutput, calls=%fused_computation.28 | convolution fusion | flops 402653184 | bytes 16777472 | tf_op jit(solution)/shard_map/japb,kapb->jk/dot_general | solution.py:58
  472.5 43.3 %fusion.32 = f32[8]{0:T(128)S(1)} fusion(f32[8,128,4,1024]{3,2,1,0:T(4,128)} %param.12, f32[128,4,1024,1]{2,0,1,3:T(8,128)} %bitcast.90), kind=kOutput, calls=%fused_computation.29 | convolution fusion | flops 50331648 | bytes 18874400 | tf_op jit(solution)/shard_map/japb,apb->j/dot_general | solution.py:60
  515.8 1.1 multiply_reduce_fusion
  517.0 39.9 %all-reduce = (f32[8,8]{1,0:T(8,128)S(1)}, f32[8]{0:T(128)S(1)}, f32[]{:T(128)}) all-reduce(f32[8,8]{1,0:T(8,128)S(1)} %fusion.29, f32[8]{0:T(128)S(1)} %fusion.32, f32[]{:T(128)} %multiply_reduce_fusion), channel_id=1, replica_groups=mesh['blk'=16,'cuts'=2] {'blk','cuts'}, use_global_device_ids=true, to_apply=%region_2.0 | all-reduce | flops 73 | bytes 584 | tf_op jit(solution)/shard_map/psum | solution.py:59
  556.9 0.6 fusion.45
  559.5 0.9 multiply_reduce_fusion.3
  560.3 0.7 fusion.44
  561.7 0.7 multiply_reduce_fusion.4
  562.3 30.8 %fusion.6 = f32[1,128,4,1024]{3,0,2,1:T(1,128)} fusion(f32[8,128,4,1024]{3,2,1,0:T(4,128)} %param.12, f32[8]{0:T(128)S(1)} %get-tuple-element.21), kind=kOutput, calls=%fused_computation.7 | convolution fusion | flops 50331648 | bytes 18874400 | tf_op jit(solution)/shard_map/j,japb->apb/dot_general | solution.py:86
  593.1 0.7 multiply_reduce_fusion.1
  598.4 6.9 %fusion.27 = f32[128,4,1024]{2,0,1:T(8,128)S(1)} fusion(f32[1,128,4,1024]{3,2,1,0:T(4,128)} %get-tuple-element.23, f32[128,4,1024]{2,0,1:T(8,128)S(1)} %copy-done.2, f32[1,128,4,1024]{3,0,2,1:T(1,128)} %fusion.6, f32[1,128,4,1024]{3,2,1,0:T(4,128)} %copy-done.3, f32[]{:T(128)} %sqrt.3, f32[]{:T(128)S(6)} %copy.114, f32[]{:T(128)} %bitcast.27), kind=kLoop, calls=%fused_computation.21 | loop fusion | flops 3145728 | bytes 10485772 | tf_op jit(solution)/shard_map/div | solution.py:90
  605.3 2.7 copy.56
  (24 shorter events, 0.2 us)
Async XLA Ops:
  7.2 49.4 %copy-start = (f32[8,8,2,2]{1,3,2,0:T(2,128)S(1)}, f32[8,8,2,2]{1,3,2,0:T(2,128)}, u32[]{:S(2)}) copy-start(f32[8,8,2,2]{1,3,2,0:T(2,128)} %param.10) | copy-start | bytes 3076
  7.2 137.3 %all-gather.9.cloned.1.call-start = ((), (), s32[]{:S(2)}) async-start(), calls=%async_computation.5 | async-start | bytes 17825792 | tf_op jit(solution)/shard_map/all_gather | solution.py:35
  11.7 1.3 copy-start.3
  11.7 3.5 copy-start.4
  15.2 185.8 %all-gather.5.cloned.1.call-start = ((), (), s32[]{:S(2)}) async-start(), calls=%async_computation.2 | async-start | bytes 6291456 | tf_op jit(solution)/shard_map/all_gather | solution.py:28
  17.8 352.9 %all-gather.7.cloned.1.call-start = ((), (), s32[]{:S(2)}) async-start(), calls=%async_computation.3 | async-start | bytes 35651584 | tf_op jit(solution)/shard_map/all_gather | solution.py:47
  53.6 2.8 copy-start.6
  53.6 2.8 copy-start.7
  56.3 416.2 %reduce-scatter.2.cloned.1.call-start = ((), (), s32[]{:S(2)}) async-start(), calls=%async_computation.4 | async-start | bytes 6291456 | tf_op jit(solution)/shard_map/reduce_scatter | solution.py:52
  201.0 25.6 %copy-start.5 = (f32[8,8,2,2,2,2]{1,0,5,4,3,2:T(8,128)S(1)}, f32[8,8,2,2,2,2]{1,0,5,4,3,2:T(8,128)}, u32[]{:S(2)}) copy-start(f32[8,8,2,2,2,2]{1,0,5,4,3,2:T(8,128)} %copy.48) | copy-start | bytes 12292
  472.5 43.3 %copy-start.2 = (f32[128,4,1024]{2,0,1:T(8,128)S(1)}, f32[128,4,1024]{2,0,1:T(8,128)}, u32[]{:S(2)}) copy-start(f32[128,4,1024]{2,0,1:T(8,128)} %reduce-scatter.2.cloned.1.call-done) | copy-start | bytes 6291460
  598.4 9.6 %copy-start.1 = (f32[8,8,2,2]{1,3,2,0:T(2,128)S(1)}, f32[8,8,2,2]{1,3,2,0:T(2,128)}, u32[]{:S(2)}) copy-start(f32[8,8,2,2]{1,3,2,0:T(2,128)} %param.10) | copy-start | bytes 3076
Sparse Core Ops, SparseCore 0:
  15.3 129.1 all-gather.8
  146.0 54.8 all-gather.4
  202.5 168.0 all-gather.6
  417.5 54.3 reduce-scatter.1
where the time goes:
time: 624 us; the launch traced here: 616 us
  waiting for transfers between devices  245 us (39%)
  matrix products  222 us (36%)
  blocking collectives  70.2 us (11%)
  local copies, waits for them, and re-layouts  45.5 us (7%)
  between operations  23.3 us (4%)
  other arithmetic  10.3 us (2%)
    all_gather x1, waiting for transfers between devices, on_device(): block_rows = lax.all_gather(right_local, 'blk', axis=0, tiled=True)  123 us
    all_gather x1, waiting for transfers between devices, on_device(): block_rows = lax.all_gather(current, 'blk', axis=0, tiled=True)  87.1 us
    dot_general x1, matrix products, on_device(): jnp.einsum('japb,kapb->jk', krylov_basis, krylov_basis, precision=highest)  54.5 us
    dot_general x1, matrix products, on_device(): lax.dot_general(left_side, flat_rows, (((1,), (1,)), ((), ())), preferred...  46.7 us
    dot_general x1, matrix products, on_device(): jnp.einsum('japb,apb->j', krylov_basis, image_vec, precision=highest)  43.3 us
    psum x1, blocking collectives, on_device(): gram_matrix = lax.psum(local_gram, ('blk', 'cuts')) / entries  39.9 us
    all_gather x1, waiting for transfers between devices, on_device(): left_full = lax.all_gather(left_env, 'cuts', axis=1, tiled=True)  34.2 us
    dot_general x1, matrix products, on_device(): jnp.einsum('j,japb->apb', ortho_coeffs, krylov_basis, precision=highest)  30.8 us
  transfers between devices with their start and end apart: 4, of which 3 were waited for; matrix products, arithmetic and copies ran while one was open for 22% of the time, Pallas kernels for 0%

commit v1 on v0

v1 whole, which is shorter than its diff:
```python
import functools

import jax
import jax.numpy as jnp
from jax import lax
from jax.experimental import pallas as pl
from jax.experimental.pallas import tpu as pltpu
from jax.sharding import PartitionSpec as P

VMEM_BYTES = 60 * 1024 * 1024


def params():
    return pltpu.CompilerParams(vmem_limit_bytes=VMEM_BYTES)


def tile_of(size, most):
    return most if size % most == 0 else size


def build_table(left_core, right_core, slot_bond):
    bond_width = left_core.shape[0]
    phys_dim = left_core.shape[2]
    chosen = (slot_bond[:, None] == jnp.arange(bond_width, dtype=jnp.int32)[None, :]).astype(
        jnp.float32
    )
    picked = jnp.einsum("kw,wxac->kxac", chosen, left_core, precision=lax.Precision.HIGHEST)
    table = jnp.einsum("kxac,xybd->kyabcd", picked, right_core, precision=lax.Precision.HIGHEST)
    return table.reshape(bond_width, bond_width, phys_dim * phys_dim, phys_dim * phys_dim)


def mix_kernel(mix_ref, left_ref, cur_ref, out_ref, proj):
    slots, rows, depth = left_ref.shape
    pairs = cur_ref.shape[0]
    bonds = out_ref.shape[0]
    cols = cur_ref.shape[2]

    @pl.loop(0, pairs)
    def _(q):
        proj[q] = jnp.dot(
            left_ref[...].reshape(slots * rows, depth),
            cur_ref[q],
            preferred_element_type=jnp.float32,
        ).reshape(slots, rows, cols)

    @pl.loop(0, rows // 16)
    def _(g):
        mixed = []
        for h in range(2):
            at = pl.ds(pl.multiple_of(g * 16 + h * 8, 8), 8)
            stacked = jnp.concatenate(
                [proj[q, k, at, :] for k in range(slots) for q in range(pairs)], axis=0
            )
            mixed.append(
                jnp.dot(
                    mix_ref[...],
                    stacked,
                    precision=lax.Precision.HIGHEST,
                    preferred_element_type=jnp.float32,
                )
            )
        at = pl.ds(pl.multiple_of(g * 16, 16), 16)
        for y in range(bonds):
            for p in range(pairs):
                i = (y * pairs + p) * 8
                out_ref[y, p, at, :] = jnp.concatenate(
                    [m[i : i + 8] for m in mixed], axis=0
                ).astype(out_ref.dtype)


def mixed_left_of(table, left_k, cur_full):
    slots, rows, depth = left_k.shape
    pairs, _, cols = cur_full.shape
    bonds = table.shape[1]
    tb = tile_of(cols, 256)
    square = table.transpose(1, 2, 0, 3).reshape(bonds * pairs, slots * pairs)
    mix = jnp.kron(square, jnp.eye(8, dtype=jnp.float32))
    return pl.pallas_call(
        mix_kernel,
        grid=(cols // tb,),
        in_specs=[
            pl.BlockSpec(mix.shape, lambda i: (0, 0)),
            pl.BlockSpec((slots, rows, depth), lambda i: (0, 0, 0)),
            pl.BlockSpec((pairs, depth, tb), lambda i: (0, 0, i)),
        ],
        out_specs=pl.BlockSpec((bonds, pairs, rows, tb), lambda i: (0, 0, 0, i)),
        out_shape=jax.ShapeDtypeStruct((bonds, pairs, rows, cols), jnp.bfloat16),
        scratch_shapes=[pltpu.VMEM((pairs, slots, rows, tb), jnp.float32)],
        compiler_params=params(),
        cost_estimate=pl.CostEstimate(
            flops=2 * slots * rows * depth * pairs * cols,
            bytes_accessed=2 * (left_k.size + cur_full.size + bonds * pairs * rows * cols),
            transcendentals=0,
        ),
    )(mix, left_k, cur_full)


def image_kernel(start_ref, mixed_ref, right_ref, out_ref):
    bonds = mixed_ref.shape[0]
    out_ref[...] = jnp.zeros_like(out_ref)

    @pl.loop(0, bonds)
    def _(y):
        out_ref[...] += lax.dot_general(
            mixed_ref[y],
            right_ref[y],
            (((1,), (1,)), ((), ())),
            preferred_element_type=jnp.float32,
        )


def image_part(mixed, right_full, start, count):
    bonds, lines, cols = mixed.shape
    tb = tile_of(count, 256)
    return pl.pallas_call(
        image_kernel,
        grid_spec=pltpu.PrefetchScalarGridSpec(
            num_scalar_prefetch=1,
            grid=(count // tb,),
            in_specs=[
                pl.BlockSpec((bonds, lines, cols), lambda i, s: (0, 0, 0)),
                pl.BlockSpec((bonds, tb, cols), lambda i, s: (0, s[0] + i, 0)),
            ],
            out_specs=pl.BlockSpec((lines, tb), lambda i, s: (0, i)),
        ),
        out_shape=jax.ShapeDtypeStruct((lines, count), jnp.float32),
        compiler_params=params(),
        cost_estimate=pl.CostEstimate(
            flops=2 * bonds * lines * cols * count,
            bytes_accessed=2 * (mixed.size + bonds * count * cols),
            transcendentals=0,
        ),
    )((start // tb).reshape(1).astype(jnp.int32), mixed, right_full)


def gram_kernel(basis_ref, out_ref):
    basis_count, rows, pairs, cols = basis_ref.shape
    chunk = 4
    lanes = cols // 128

    @pl.when(pl.program_id(0) == 0)
    def _():
        out_ref[...] = jnp.zeros_like(out_ref)

    @pl.loop(0, rows // chunk)
    def _(r):
        for c in range(lanes):
            vecs = [
                basis_ref[j, pl.ds(r * chunk, chunk), :, c * 128 : (c + 1) * 128]
                for j in range(basis_count)
            ]
            i = 0
            for j in range(basis_count):
                for k in range(j, basis_count):
                    out_ref[i] += jnp.sum(vecs[j] * vecs[k], axis=0)
                    i += 1


def gram_of(basis):
    basis_count, rows, pairs, cols = basis.shape
    count = basis_count * (basis_count + 1) // 2
    ta = tile_of(rows, 16)
    sums = pl.pallas_call(
        gram_kernel,
        grid=(rows // ta,),
        in_specs=[pl.BlockSpec((basis_count, ta, pairs, cols), lambda i: (0, i, 0, 0))],
        out_specs=pl.BlockSpec((count, pairs, 128), lambda i: (0, 0, 0)),
        out_shape=jax.ShapeDtypeStruct((count, pairs, 128), jnp.float32),
        compiler_params=params(),
        cost_estimate=pl.CostEstimate(
            flops=2 * count * rows * pairs * cols,
            bytes_accessed=4 * basis.size,
            transcendentals=0,
        ),
    )(basis)
    return jnp.sum(sums, axis=(1, 2))


def dots_kernel(basis_ref, image_ref, out_ref):
    basis_count, rows, pairs, cols = basis_ref.shape

    @pl.when(pl.program_id(0) == 0)
    def _():
        out_ref[...] = jnp.zeros_like(out_ref)

    for c in range(cols // 128):
        at = slice(c * 128, (c + 1) * 128)
        image = image_ref[:, :, at]
        for j in range(basis_count):
            out_ref[j] += jnp.sum(basis_ref[j, :, :, at] * image, axis=0)
        out_ref[basis_count] += jnp.sum(image * image, axis=0)


def dots_of(basis, image):
    basis_count, rows, pairs, cols = basis.shape
    ta = tile_of(rows, 16)
    sums = pl.pallas_call(
        dots_kernel,
        grid=(rows // ta,),
        in_specs=[
            pl.BlockSpec((basis_count, ta, pairs, cols), lambda i: (0, i, 0, 0)),
            pl.BlockSpec((ta, pairs, cols), lambda i: (i, 0, 0)),
        ],
        out_specs=pl.BlockSpec((basis_count + 1, pairs, 128), lambda i: (0, 0, 0)),
        out_shape=jax.ShapeDtypeStruct((basis_count + 1, pairs, 128), jnp.float32),
        compiler_params=params(),
    )(basis, image)
    return jnp.sum(sums, axis=(1, 2))


def final_kernel(coef_ref, basis_ref, image_ref, out_ref):
    basis_count = basis_ref.shape[0]
    total = image_ref[...]
    for j in range(basis_count):
        total = total - coef_ref[j] * basis_ref[j]
    out_ref[...] = total * coef_ref[basis_count]


def final_of(coefs, basis, image):
    basis_count, rows, pairs, cols = basis.shape
    ta = tile_of(rows, 16)
    return pl.pallas_call(
        final_kernel,
        grid=(rows // ta,),
        in_specs=[
            pl.BlockSpec(memory_space=pltpu.SMEM),
            pl.BlockSpec((basis_count, ta, pairs, cols), lambda i: (0, i, 0, 0)),
            pl.BlockSpec((ta, pairs, cols), lambda i: (i, 0, 0)),
        ],
        out_specs=pl.BlockSpec((ta, pairs, cols), lambda i: (i, 0, 0)),
        out_shape=jax.ShapeDtypeStruct((rows, pairs, cols), jnp.float32),
        compiler_params=params(),
    )(coefs, basis, image)


def on_device(
    cuts, left_env, right_env, left_core, right_core, slot_bond, krylov_basis, beta_prev
):
    bond_width = left_core.shape[0]
    pair_count = left_core.shape[2] * left_core.shape[2]
    basis_count, row_count, _, col_count = krylov_basis.shape
    full_width = left_env.shape[2]
    entries = float(full_width * pair_count * full_width)
    table = build_table(left_core, right_core, slot_bond)
    me = lax.axis_index("cuts")
    swap = [(0, 1), (1, 0)]

    current = krylov_basis[basis_count - 1].astype(jnp.bfloat16).transpose(1, 0, 2)
    left_t = left_env.transpose(1, 0, 2)
    right_t = right_env.transpose(1, 0, 2)
    if cuts == 2:
        half = left_t.shape[0]
        theirs = lax.dynamic_slice_in_dim(right_t, (1 - me) * col_count, col_count, 2)
        mine = lax.dynamic_slice_in_dim(right_t, me * col_count, col_count, 2)
        right_k = jnp.concatenate([mine, lax.ppermute(theirs, "cuts", swap)], axis=0)
        left_k = jnp.concatenate([left_t, lax.ppermute(left_t, "cuts", swap)], axis=0)
        turned = jnp.roll(jnp.roll(table, -half, axis=0), -half, axis=1)
        table = jnp.where(me == 0, table, turned)
    else:
        left_k = lax.all_gather(left_t, "cuts", axis=0, tiled=True)
        right_k = lax.all_to_all(right_t, "cuts", split_axis=2, concat_axis=0, tiled=True)
    cur_full = lax.all_gather(current, "blk", axis=1, tiled=True)
    right_full = lax.all_gather(right_k, "blk", axis=1, tiled=True)
    gram = gram_of(krylov_basis)

    mixed = mixed_left_of(table, left_k, cur_full)
    mixed = mixed.reshape(bond_width, pair_count * row_count, col_count)
    if cuts == 2:
        away = image_part(mixed, right_full, (1 - me) * col_count, col_count)
        away = lax.ppermute(away, "cuts", swap)
        here = image_part(mixed, right_full, me * col_count, col_count)
        image = here + away
    else:
        image = image_part(mixed, right_full, jnp.int32(0), full_width)
        image = lax.psum_scatter(image, "cuts", scatter_dimension=1, tiled=True)
    image = image.reshape(pair_count, row_count, col_count).transpose(1, 0, 2)

    sums = lax.psum(jnp.concatenate([gram, dots_of(krylov_basis, image)]), ("blk", "cuts"))
    sums = sums / entries
    count = basis_count * (basis_count + 1) // 2
    where = []
    for j in range(basis_count):
        for k in range(basis_count):
            low, high = min(j, k), max(j, k)
            where.append(low * basis_count - low * (low - 1) // 2 + high - low)
    gram_matrix = sums[jnp.array(where)].reshape(basis_count, basis_count)
    inner_prods = sums[count : count + basis_count]
    image_square = sums[count + basis_count]
    last, prior = basis_count - 1, basis_count - 2
    alpha_now = inner_prods[last]
    ortho_coeffs = (
        inner_prods - alpha_now * gram_matrix[:, last] - beta_prev * gram_matrix[:, prior]
    )
    first_square = (
        image_square
        - 2.0 * alpha_now * inner_prods[last]
        - 2.0 * beta_prev * inner_prods[prior]
        + alpha_now * alpha_now * gram_matrix[last, last]
        + 2.0 * alpha_now * beta_prev * gram_matrix[last, prior]
        + beta_prev * beta_prev * gram_matrix[prior, prior]
    )
    square_mean = (
        first_square
        - 2.0 * jnp.sum(ortho_coeffs * ortho_coeffs)
        + jnp.sum(ortho_coeffs[:, None] * gram_matrix * ortho_coeffs[None, :])
    )
    beta_new = jnp.sqrt(square_mean + 1e-06)
    index = jnp.arange(basis_count)
    coefs = (
        ortho_coeffs
        + jnp.where(index == last, alpha_now, 0.0)
        + jnp.where(index == prior, beta_prev, 0.0)
    )
    coefs = jnp.concatenate([coefs, (1.0 / beta_new)[None]])
    next_vector = final_of(coefs, krylov_basis, image)
    return (next_vector, alpha_now[None], beta_new[None])


def solution(mesh):
    in_specs = (
        P("blk", "cuts", None),
        P("blk", "cuts", None),
        P(),
        P(),
        P(),
        P(None, "blk", None, "cuts"),
        P(),
    )
    out_specs = (P("blk", None, "cuts"), P(), P())
    return jax.shard_map(
        functools.partial(on_device, mesh.shape["cuts"]),
        mesh=mesh,
        in_specs=in_specs,
        out_specs=out_specs,
        check_vma=False,
    )
```

time: 624 us -> 464 us (0.74); the launches traced: 616 us -> 463 us
  matrix products: 222 us -> 0.38 us
  Pallas kernels: 0 us -> 124 us
  blocking collectives: 70.2 us -> 39.8 us
  local copies, waits for them, and re-layouts: 45.5 us -> 18.3 us
  waiting for transfers between devices: 245 us -> 235 us
  starting transfers between devices: 0.16 us -> 6.41 us
    dot_general x6 -> x0, matrix products: 222 us -> none  [the longest x1 54.5 us: on_device(): jnp.einsum('japb,kapb->jk', krylov_basis, krylov_basis, precision=highest)]
    pallas_call x0 -> x6, Pallas kernels: none -> 124 us  [the longest x1 44.8 us: mixed_left_of(): pl.pallas_call(mix_kernel, grid=(cols // tb,), in_specs=[pl.BlockSpec(mix...]
    all_gather x3 -> x2, waiting for transfers between devices: 245 us -> 169 us  [the longest x1 124 us: on_device(): right_full = lax.all_gather(right_k, 'blk', axis=1, tiled=True)]
    ppermute x0 -> x3, waiting for transfers between devices: none -> 65.9 us  [the longest x1 36.8 us: on_device(): lax.ppermute(left_t, 'cuts', swap)]
    all_to_all x1 -> x0, blocking collectives: 30.2 us -> none  [on_device(): lax.all_to_all(right_env, 'cuts', split_axis=2, concat_axis=1, tiled=True)]
    all_gather x1 -> x0, local copies, waits for them, and re-layouts: 22.2 us -> none  [on_device(): block_rows = lax.all_gather(current, 'blk', axis=0, tiled=True)]
    unnamed x20 -> x16, local copies, waits for them, and re-layouts: 14.2 us -> 5.3 us
    div x3 -> x1, other arithmetic: 6.92 us -> 0.01 us  [on_device(): sums = sums / entries]
  transfers between devices with their start and end apart: 4 -> 5, of which waited for: 3 -> 5; matrix products, arithmetic and copies ran while one was open for 22% -> 4% of each run, Pallas kernels for 0% -> 18%
where the time goes in v1:
time: 464 us; the launch traced here: 463 us
  waiting for transfers between devices  235 us (51%)
  Pallas kernels  124 us (27%)
  blocking collectives  39.8 us (9%)
  between operations  23 us (5%)
  local copies, waits for them, and re-layouts  18.3 us (4%)
  other arithmetic  16 us (3%)
  starting transfers between devices  6.41 us (1%)
    all_gather x1, waiting for transfers between devices, on_device(): right_full = lax.all_gather(right_k, 'blk', axis=1, tiled=True)  124 us
    all_gather x1, waiting for transfers between devices, on_device(): cur_full = lax.all_gather(current, 'blk', axis=1, tiled=True)  45.9 us
    pallas_call x1, Pallas kernels, mixed_left_of(): pl.pallas_call(mix_kernel, grid=(cols // tb,), in_specs=[pl.BlockSpec(mix...  44.8 us
    pallas_call x2, Pallas kernels, image_part(): pl.pallas_call(image_kernel, grid_spec=pltpu.PrefetchScalarGridSpec(num_s...  41.8 us
    psum x1, blocking collectives, on_device(): lax.psum(jnp.concatenate([gram, dots_of(krylov_basis, image)]), ('blk', '...  39.8 us
    ppermute x1, waiting for transfers between devices, on_device(): lax.ppermute(left_t, 'cuts', swap)  36.8 us
    ppermute x1, waiting for transfers between devices, on_device(): lax.ppermute(theirs, 'cuts', swap)  22.8 us
    pallas_call x1, Pallas kernels, gram_of(): pl.pallas_call(gram_kernel, grid=(rows // ta,), in_specs=[pl.BlockSpec((b...  17.4 us
  transfers between devices with their start and end apart: 5, of which 5 were waited for; matrix products, arithmetic and copies ran while one was open for 4% of the time, Pallas kernels for 18%

profile of v1, /device:TPU:0, one launch (start us, length us, event | category | flops | bytes accessed | tf_op | source)
XLA Modules:
  0.0 463.4 jit_solution(4286294273900218205)
XLA Ops:
  7.2 2.1 slice.78
  9.3 1.3 copy.50
  11.3 1.0 constant_dynamic-slice_fusion.1
  12.6 3.1 collective-permute-start.1
  16.0 22.8 %collective-permute-done.1 = bf16[4,128,1024]{2,1,0:T(8,128)(2,1)S(1)} collective-permute-done((bf16[4,128,1024]{2,1,0:T(8,128)(2,1)S(1)}, bf16[4,128,1024]{2,1,0:T(8,128)(2,1)S(1)}, u32[]{:S(2)}, u32[]{:S(2)}) %collective-permute-start.1) | collective-permute-done | bytes 1048608 | tf_op jit(solution)/shard_map/ppermute | solution.py:255
  38.8 1.5 pad_maximum_fusion.1
  40.4 2.8 copy.49
  43.1 1.8 collective-permute-start
  46.1 2.6 broadcast_multiply_fusion
  48.7 4.7 %mul.122.mix_ref = f32[256,256]{1,0:T(8,128)} reshape(f32[32,8,32,8]{3,2,1,0:T(8,128)} %broadcast_multiply_fusion) | data formatting | bytes 524288 | tf_op jit(solution)/shard_map/jit(kron)/mul | solution.py:77
  53.4 36.8 %collective-permute-done = bf16[4,128,2048]{2,1,0:T(8,128)(2,1)} collective-permute-done((bf16[4,128,2048]{2,1,0:T(8,128)(2,1)S(1)}, bf16[4,128,2048]{2,1,0:T(8,128)(2,1)}, u32[]{:S(2)}, u32[]{:S(2)}) %collective-permute-start) | collective-permute-done | bytes 2097184 | tf_op jit(solution)/shard_map/ppermute | solution.py:256
  90.2 3.9 pad_maximum_fusion.left_ref
  94.1 45.9 %all-gather.3.cloned.1.call-done.cur_ref = bf16[4,2048,1024]{2,1,0:T(8,128)(2,1)} async-done(((bf16[4,128,1024]{2,1,0:T(8,128)(2,1)}), bf16[4,2048,1024]{2,1,0:T(8,128)(2,1)}) %all-gather.3.cloned.1.call-update) | async-done | bytes 16777232 | tf_op jit(solution)/shard_map/all_gather | solution.py:262
  140.0 44.8 %shard_map.104 = bf16[8,4,128,1024]{3,2,1,0:T(8,128)(2,1)} custom-call(f32[256,256]{1,0:T(8,128)} %mul.122.mix_ref, bf16[8,128,2048]{2,1,0:T(8,128)(2,1)} %pad_maximum_fusion.left_ref, bf16[4,2048,1024]{2,1,0:T(8,128)(2,1)} %all-gather.3.cloned.1.call-done.cur_ref), custom_call_target="tpu_custom_call" | custom-call | flops 17179869184 | bytes 29360128 | tf_op jit(solution)/shard_map/pallas_call | solution.py:78
  184.8 123.5 %all-gather.5.cloned.1.call-done.right_ref = bf16[8,2048,1024]{2,1,0:T(8,128)(2,1)} async-done(((bf16[8,128,1024]{2,1,0:T(8,128)(2,1)}), bf16[8,2048,1024]{2,1,0:T(8,128)(2,1)}) %all-gather.5.cloned.1.call-update) | async-done | bytes 33554448 | tf_op jit(solution)/shard_map/all_gather | solution.py:263
  308.4 20.9 %shard_map.106 = f32[512,1024]{1,0:T(8,128)} custom-call(s32[1]{0:T(128)} %bitcast.17.start_ref, bf16[8,512,1024]{2,1,0:T(8,128)(2,1)} %bitcast.52, bf16[8,2048,1024]{2,1,0:T(8,128)(2,1)} %all-gather.5.cloned.1.call-done.right_ref), custom_call_target="tpu_custom_call" | custom-call | flops 8589934592 | bytes 25165824 | tf_op jit(solution)/shard_map/pallas_call | solution.py:115
  329.3 1.5 collective-permute-start.2
  331.4 17.4 %shard_map.103 = f32[36,4,128]{2,1,0:T(4,128)} custom-call(f32[8,128,4,1024]{3,2,1,0:T(4,128)} %basis_ref.5), custom_call_target="tpu_custom_call" | custom-call | flops 37748736 | bytes 16777216 | tf_op jit(solution)/shard_map/pallas_call | solution.py:163
  348.8 1.2 reduce_sum.36
  350.1 20.9 %shard_map.105 = f32[512,1024]{1,0:T(8,128)} custom-call(s32[1]{0:T(128)} %bitcast.start_ref, bf16[8,512,1024]{2,1,0:T(8,128)(2,1)} %bitcast.53, bf16[8,2048,1024]{2,1,0:T(8,128)(2,1)} %all-gather.5.cloned.1.call-done.right_ref), custom_call_target="tpu_custom_call" | custom-call | flops 8589934592 | bytes 25165824 | tf_op jit(solution)/shard_map/pallas_call | solution.py:115
  371.0 6.3 %collective-permute-done.2 = f32[512,1024]{1,0:T(8,128)S(1)} collective-permute-done((f32[512,1024]{1,0:T(8,128)}, f32[512,1024]{1,0:T(8,128)S(1)}, u32[]{:S(2)}, u32[]{:S(2)}) %collective-permute-start.2) | collective-permute-done | bytes 2097184 | tf_op jit(solution)/shard_map/ppermute | solution.py:270
  377.3 2.0 add.42
  379.3 2.7 copy.48
  382.0 10.7 %shard_map.107 = f32[9,4,128]{2,1,0:T(4,128)} custom-call(f32[8,128,4,1024]{3,2,1,0:T(4,128)} %basis_ref.5, f32[128,4,1024]{2,1,0:T(4,128)} %bitcast.54), custom_call_target="tpu_custom_call" | custom-call | tf_op jit(solution)/shard_map/pallas_call | solution.py:197
  392.7 0.9 reduce_sum.37
  393.6 39.8 %psum.7 = f32[45]{0:T(128)S(1)} all-reduce(f32[45]{0:T(128)S(1)} %pad_maximum_fusion.3), channel_id=1, replica_groups=mesh['blk'=16,'cuts'=2] {'blk','cuts'}, use_global_device_ids=true, to_apply=%region_2.3 | all-reduce | flops 45 | bytes 360 | tf_op jit(solution)/shard_map/psum | solution.py:278
  436.6 0.8 gather_fusion
  437.4 0.6 fusion.13
  438.1 0.9 multiply_reduce_fusion.2
  438.9 0.7 fusion.11
  440.3 0.7 multiply_reduce_fusion
  446.0 9.4 %shard_map.108 = f32[128,4,1024]{2,1,0:T(4,128)} custom-call(f32[9]{0:T(128)} %pad_maximum_fusion.4.coef_ref, f32[8,128,4,1024]{3,2,1,0:T(4,128)} %basis_ref.5, f32[128,4,1024]{2,1,0:T(4,128)} %bitcast.55), custom_call_target="tpu_custom_call" | custom-call | tf_op jit(solution)/shard_map/pallas_call | solution.py:222
  (38 shorter events, 4.4 us)
Async XLA Ops:
  7.2 38.0 %copy-start = (f32[8,8,2,2]{1,3,2,0:T(2,128)S(1)}, f32[8,8,2,2]{1,3,2,0:T(2,128)}, u32[]{:S(2)}) copy-start(f32[8,8,2,2]{1,3,2,0:T(2,128)} %param.11) | copy-start | bytes 3076
  7.2 132.8 %all-gather.3.cloned.1.call-start = ((), (), s32[]{:S(2)}) async-start(), calls=%async_computation | async-start | bytes 17825792 | tf_op jit(solution)/shard_map/all_gather | solution.py:262
  9.3 2.0 copy-start.2
  10.7 297.7 %all-gather.5.cloned.1.call-start = ((), (), s32[]{:S(2)}) async-start(), calls=%async_computation.1 | async-start | bytes 35651584 | tf_op jit(solution)/shard_map/all_gather | solution.py:263
  12.6 26.2 %collective-permute-start.1 = (bf16[4,128,1024]{2,1,0:T(8,128)(2,1)S(1)}, bf16[4,128,1024]{2,1,0:T(8,128)(2,1)S(1)}, u32[]{:S(2)}, u32[]{:S(2)}) collective-permute-start(bf16[4,128,1024]{2,1,0:T(8,128)(2,1)S(1)} %bitcast.61), channel_id=1, source_target_pairs={{0,1},{1,0},{2,3},{3,2},{4,5},{5,4},{6,7},{7,6},{8,9},{9,8},{10,11... | collective-permute-start | bytes 3145736 | tf_op jit(solution)/shard_map/ppermute | solution.py:255
  40.4 4.6 copy-start.4
  40.4 4.6 copy-start.5
  43.1 47.1 %collective-permute-start = (bf16[4,128,2048]{2,1,0:T(8,128)(2,1)S(1)}, bf16[4,128,2048]{2,1,0:T(8,128)(2,1)}, u32[]{:S(2)}, u32[]{:S(2)}) collective-permute-start(bf16[4,128,2048]{2,1,0:T(8,128)(2,1)S(1)} %bitcast.57), channel_id=1, source_target_pairs={{0,1},{1,0},{2,3},{3,2},{4,5},{5,4},{6,7},{7,6},{8,9},{9,8},{10,11... | collective-permute-start | bytes 6291464 | tf_op jit(solution)/shard_map/ppermute | solution.py:256
  329.3 48.0 %collective-permute-start.2 = (f32[512,1024]{1,0:T(8,128)}, f32[512,1024]{1,0:T(8,128)S(1)}, u32[]{:S(2)}, u32[]{:S(2)}) collective-permute-start(f32[512,1024]{1,0:T(8,128)} %shard_map.106), channel_id=1, source_target_pairs={{0,1},{1,0},{2,3},{3,2},{4,5},{5,4},{6,7},{7,6},{8,9},{9,8},{10,11... | collective-permute-start | bytes 6291464 | tf_op jit(solution)/shard_map/ppermute | solution.py:270
  331.4 18.7 %copy-start.3 = (s32[64]{0:T(128)S(1)}, s32[64]{0:T(128)}, u32[]{:S(2)}) copy-start(s32[64]{0:T(128)} %constant.58) | copy-start | bytes 772
  446.0 9.4 %copy-start.1 = (f32[8,8,2,2]{1,3,2,0:T(2,128)S(1)}, f32[8,8,2,2]{1,3,2,0:T(2,128)}, u32[]{:S(2)}) copy-start(f32[8,8,2,2]{1,3,2,0:T(2,128)} %param.11) | copy-start | bytes 3076
Sparse Core Ops, SparseCore 0:
  10.8 129.1 all-gather.2
  142.1 166.2 all-gather.4
